TPU v7x, 32 devices: a whole 2x2x4 slice. The times are simulated.
32 devices in a mesh: segment: 4 (over y, core), dp: 8 (over z, x).
Axes of the slice: x: 2, y: 2, z: 4, core: 2. Of those that a mesh axis runs over, the one named last changes fastest.
Arguments:
- token_ids: int32 [1024], P('dp'), may hold values from 0 to 38015, as said below
- table: bfloat16 [4752, 28672], P('segment', 'dp'), may hold values from -6 to 6
- out_grad: bfloat16 [1024, 3584], P('dp', 'segment'), may hold values from -6 to 6
Outputs:
- embedded: bfloat16 [1024, 3584], P('dp')
- table_grad: bfloat16 [4752, 28672], P('segment', 'dp')
Inputs may be any that keep to these rules, and one draw needn't show every extreme that they name: `token_ids`: in the 128 tokens of each data group, at most 16 ids lie in one segment's slice of 9504 rows with one residue modulo 8; in every data group some segment and residue has exactly 16.
All inputs are finite; a program needn't handle non-finite values.
Results may differ from a plain program's by a relative error of at most 0.001.
Values may be sent and summed in bfloat16 or wider, within the bound.
A program may use at most 64 MiB of HBM per device.

v0:
```python
import jax
import jax.numpy as jnp
from jax import lax
from jax.sharding import PartitionSpec as P

D = 3584
PACK = 8


def body(token_ids, table, out_grad):
    lines = table.shape[0]
    width = table.shape[1]
    groups = lax.axis_size("dp")
    tok_rows = token_ids.shape[0]
    quarters = D // width
    slot = lax.axis_index("dp") // quarters
    first = lax.axis_index("segment") * lines * PACK
    every_id = lax.all_gather(token_ids, "dp", axis=0, tiled=True)
    local = every_id - first
    in_section = (local >= 0) & (local < lines * PACK)
    owned = in_section & (local % PACK == slot)
    line_idx = jnp.clip(local // PACK, 0, lines - 1)
    whole_grad = lax.all_gather(out_grad, "segment", axis=1, tiled=True)
    capacity = tok_rows // PACK
    owned_grid = owned.reshape(groups, tok_rows)
    rank = jnp.cumsum(owned_grid.astype(jnp.int32), axis=1) - 1
    place = jnp.where(owned_grid, rank, capacity)
    group_rows = jnp.broadcast_to(jnp.arange(groups, dtype=jnp.int32)[:, None], (groups, tok_rows))
    row_of = (
        jnp.zeros((groups, capacity), jnp.int32)
        .at[group_rows, place]
        .set(line_idx.reshape(groups, tok_rows), mode="drop")
    )
    filled = jnp.zeros((groups, capacity), jnp.bool_).at[group_rows, place].set(True, mode="drop")
    fetched = jnp.take(table, row_of.reshape(-1), axis=0).reshape(groups, capacity, width)
    fetched = jnp.where(filled[:, :, None], fetched, jnp.zeros((), jnp.bfloat16))
    arrived = lax.all_to_all(fetched, "dp", split_axis=0, concat_axis=0, tiled=True)
    my_local = token_ids - first
    my_in = (my_local >= 0) & (my_local < lines * PACK)
    my_slot = my_local % PACK
    slot_hits = (my_slot[:, None] == jnp.arange(PACK, dtype=jnp.int32)[None, :]) & my_in[:, None]
    slot_ranks = jnp.cumsum(slot_hits.astype(jnp.int32), axis=0) - 1
    my_rank = jnp.sum(jnp.where(slot_hits, slot_ranks, 0), axis=1)
    sources = my_slot[:, None] * quarters + jnp.arange(quarters, dtype=jnp.int32)[None, :]
    flat_index = jnp.clip(sources * capacity + my_rank[:, None], 0, groups * capacity - 1)
    gathered = jnp.take(
        arrived.reshape(groups * capacity, width), flat_index.reshape(-1), axis=0
    ).reshape(tok_rows, D)
    segment_part = jnp.where(my_in[:, None], gathered.astype(jnp.float32), 0.0)
    slot_place = jnp.where(my_in, my_slot, PACK)
    token_at = (
        jnp.zeros((PACK, capacity), jnp.int32)
        .at[slot_place, my_rank]
        .set(jnp.arange(tok_rows, dtype=jnp.int32), mode="drop")
    )
    valid = jnp.zeros((PACK, capacity), jnp.bool_).at[slot_place, my_rank].set(True, mode="drop")
    grad_pick = jnp.take(whole_grad, token_at.reshape(-1), axis=0).reshape(
        PACK, capacity, quarters, width
    )
    grad_pick = jnp.where(valid[:, :, None, None], grad_pick, jnp.zeros((), jnp.bfloat16))
    grad_send = grad_pick.transpose(0, 2, 1, 3).reshape(groups, capacity, width)
    returned = lax.all_to_all(grad_send, "dp", split_axis=0, concat_axis=0, tiled=True)
    target = jnp.where(filled, row_of, lines)
    accum = (
        jnp.zeros((lines, width), jnp.float32)
        .at[target.reshape(-1)]
        .add(returned.reshape(-1, width).astype(jnp.float32), mode="drop")
    )
    embedded = lax.psum(segment_part.astype(jnp.bfloat16), "segment")
    return (embedded, accum.astype(jnp.bfloat16))


def solution(mesh):
    placed = (P("dp"), P("segment", "dp"), P("dp", "segment"))
    return jax.shard_map(
        body,
        mesh=mesh,
        in_specs=placed,
        out_specs=(P("dp", None), P("segment", "dp")),
        check_vma=False,
    )
```

profile of v0, /device:TPU:0, one launch (start us, length us, event | category | flops | bytes accessed | tf_op | source)
XLA Modules:
  0.0 159.1 jit_solution(7434590179938538914)
XLA Ops:
  7.2 0.0 copy-start.1
  7.2 0.0 copy-start
  7.2 22.6 %all-gather = s32[8,1,128]{2,1,0:T(1,128)S(1)} all-gather(s32[1,1,128]{2,1,0:T(1,128)} %bitcast.39), channel_id=1, replica_groups=mesh['segment'=4,'dp'=8] {'dp'}, dimensions={0}, use_global_device_ids=true | all-gather | bytes 4608 | tf_op jit(solution)/shard_map/all_gather | solution.py:18
  29.8 0.3 copy.12
  30.1 0.3 copy.13
  30.4 23.6 %compare_select_fusion = s32[8,128,1]{2,0,1:T(8,128)S(1)} fusion(pred[8,128,1]{2,0,1:T(8,128)(4,1)S(1)} %copy.13, s32[8,128,1]{2,0,1:T(8,128)S(1)} %copy.12), kind=kOutput, calls=%fused_computation.12 | output fusion | flops 135168 | bytes 9216 | tf_op jit(solution)/shard_map/jit(cumsum)/reduce_window_sum | solution.py:26
  54.0 0.2 copy.14
  54.2 0.8 multiply_reduce_fusion
  55.0 0.1 copy.19
  55.1 0.7 and_reduce_fusion
  55.8 0.1 copy.18
  56.0 4.3 %scatter_custom_fusion.4 = s32[128]{0:T(128)S(1)} fusion(s32[1024]{0:T(1024)S(1)} %bitcast.40, s32[1024]{0:T(1024)S(1)} %fusion.6, s32[]{:T(128)} %constant.70.clone.1), kind=kCustom, calls=%fused_computation.66 | custom fusion | bytes 516
  60.3 0.1 reshape.189
  60.4 4.3 %scatter_custom_fusion.3 = pred[128]{0:T(512)(128)(4,1)S(1)} fusion(s32[1024]{0:T(1024)S(1)} %bitcast.41, pred[1024]{0:T(1024)(128)(4,1)S(1)} %broadcast.224, pred[]{:T(512)} %constant.71.clone.1), kind=kCustom, calls=%fused_computation.56 | custom fusion | bytes 129
  64.8 0.1 reshape.185
  64.9 6.6 %gather_fusion = bf16[128,3584]{1,0:T(8,128)(2,1)S(1)} fusion(bf16[1188,3584]{1,0:T(8,128)(2,1)} %param.6, s32[1024]{0:T(1024)S(1)} %pad_clamp_fusion.2), kind=kCustom, calls=%fused_computation.2 | custom fusion | bytes 1835520 | tf_op jit(solution)/shard_map/jit(_take)/gather | solution.py:35
  71.4 1.1 select_select_fusion
  72.6 3.6 %all-to-all-start = ((bf16[8,16,3584]{2,1,0:T(8,128)(2,1)}), bf16[8,16,3584]{2,1,0:T(8,128)(2,1)S(1)}, u32[]{:S(2)}, u32[]{:S(2)}) async-start(bf16[8,16,3584]{2,1,0:T(8,128)(2,1)} %select_select_fusion), calls=%async_computation | async-start | bytes 1835008 | tf_op jit(solution)/shard_map/all_to_all | solution.py:37
  76.1 0.0 copy-done.1
  76.2 0.1 fusion.4
  76.3 0.2 reduce_window_sum.23
  76.4 0.2 select_reduce_fusion
  76.7 6.4 %scatter_fusion.1 = s32[8,16]{1,0:T(8,128)S(1)} fusion(s32[8,16]{1,0:T(8,128)S(1)} %broadcast.169, s32[128]{0:T(128)S(1)} %fusion.18, s32[128]{0:T(128)S(1)} %iota.14), kind=kCustom, calls=%fused_computation.4 | custom fusion | bytes 2560 | tf_op jit(solution)/shard_map/scatter | solution.py:54
  83.0 0.1 reshape.180
  83.1 0.0 copy-done
  83.2 9.5 %all_gather.7 = bf16[128,3584]{1,0:T(8,128)(2,1)S(1)} all-gather(bf16[128,896]{1,0:T(8,128)(2,1)S(1)} %copy-done), channel_id=1, replica_groups=mesh['segment'=4,'dp'=8] {'segment'}, dimensions={1}, use_global_device_ids=true | all-gather | bytes 1146880 | tf_op jit(solution)/shard_map/all_gather | solution.py:23
  92.7 1.1 gather_fusion.2
  93.8 6.5 %scatter_fusion = pred[8,16]{1,0:T(8,128)(4,1)S(1)} fusion(pred[8,16]{1,0:T(8,128)(4,1)S(1)} %broadcast.166, s32[128]{0:T(128)S(1)} %fusion.18, pred[128]{0:T(512)(128)(4,1)S(1)} %broadcast.225), kind=kCustom, calls=%fused_computation.3 | custom fusion | bytes 1408 | tf_op jit(solution)/shard_map/scatter | solution.py:56
  100.3 0.2 broadcast_select_fusion
  100.5 1.1 broadcast_select_fusion.1
  101.5 0.0 all-to-all-done
  101.5 5.9 %all-to-all-start.1 = ((bf16[8,16,3584]{2,1,0:T(8,128)(2,1)}), bf16[8,16,3584]{2,1,0:T(8,128)(2,1)S(1)}, u32[]{:S(2)}, u32[]{:S(2)}) async-start(bf16[8,16,3584]{2,1,0:T(8,128)(2,1)} %broadcast_select_fusion.1), calls=%async_computation.1 | async-start | bytes 1835008 | tf_op jit(solution)/shard_map/all_to_all | solution.py:62
  107.5 0.0 all-reduce.2.cloned.1.call-start
  107.5 1.1 gather_fusion.1
  108.7 1.3 select_convert_fusion
  109.9 0.0 all-reduce.2.cloned.1.call-update
  110.0 0.1 reshape.179
  110.1 20.9 %all-to-all-done.1 = bf16[8,16,3584]{2,1,0:T(8,128)(2,1)S(1)} async-done(((bf16[8,16,3584]{2,1,0:T(8,128)(2,1)}), bf16[8,16,3584]{2,1,0:T(8,128)(2,1)S(1)}, u32[]{:S(2)}, u32[]{:S(2)}) %all-to-all-start.1) | async-done | bytes 917536 | tf_op jit(solution)/shard_map/all_to_all | solution.py:62
  130.9 10.0 %scatter_custom_fusion.2 = f32[1188,3584]{1,0:T(8,128)} fusion(s32[128]{0:T(128)S(1)} %fusion.16, f32[]{:T(128)} %constant.121.clone.1, bf16[128,3584]{1,0:T(8,128)(2,1)S(1)} %bitcast.35), kind=kCustom, calls=%fused_computation.8 | custom fusion | flops 917504 | bytes 17948676 | tf_op jit(solution)/shard_map/scatter-add | solution.py:67
  140.9 9.1 %convert_element_type.32 = bf16[1188,3584]{1,0:T(8,128)(2,1)} convert(f32[1188,3584]{1,0:T(8,128)} %scatter_custom_fusion.2) | non-fusion elementwise | flops 4257792 | bytes 25546752 | tf_op jit(solution)/shard_map/convert_element_type | solution.py:70
  150.1 0.0 all-reduce.2.cloned.1.call-done
  150.1 2.2 %copy.23 = bf16[128,3584]{1,0:T(8,128)(2,1)} copy(bf16[128,3584]{1,0:T(8,128)(2,1)} %all-reduce.2.cloned.1.call-done) | data formatting | bytes 1835008
  (24 shorter events, 0.2 us)
Async XLA Ops:
  7.2 69.0 %copy-start.1 = (s32[128]{0:T(128)S(1)}, s32[128]{0:T(128)}, u32[]{:S(2)}) copy-start(s32[128]{0:T(128)} %param.5) | copy-start | bytes 1540
  7.2 76.0 %copy-start = (bf16[128,896]{1,0:T(8,128)(2,1)S(1)}, bf16[128,896]{1,0:T(8,128)(2,1)}, u32[]{:S(2)}) copy-start(bf16[128,896]{1,0:T(8,128)(2,1)} %param.7) | copy-start | bytes 688132
  72.6 29.0 %all-to-all-start = ((bf16[8,16,3584]{2,1,0:T(8,128)(2,1)}), bf16[8,16,3584]{2,1,0:T(8,128)(2,1)S(1)}, u32[]{:S(2)}, u32[]{:S(2)}) async-start(bf16[8,16,3584]{2,1,0:T(8,128)(2,1)} %select_select_fusion), calls=%async_computation | async-start | bytes 1835008 | tf_op jit(solution)/shard_map/all_to_all | solution.py:37
  101.5 29.4 %all-to-all-start.1 = ((bf16[8,16,3584]{2,1,0:T(8,128)(2,1)}), bf16[8,16,3584]{2,1,0:T(8,128)(2,1)S(1)}, u32[]{:S(2)}, u32[]{:S(2)}) async-start(bf16[8,16,3584]{2,1,0:T(8,128)(2,1)} %broadcast_select_fusion.1), calls=%async_computation.1 | async-start | bytes 1835008 | tf_op jit(solution)/shard_map/all_to_all | solution.py:62
  107.5 42.6 %all-reduce.2.cloned.1.call-start = ((), (), s32[]{:S(2)}) async-start(), calls=%async_computation.2 | async-start | bytes 1835008 | tf_op jit(solution)/shard_map/psum | solution.py:69
Sparse Core Ops, SparseCore 0:
  111.2 36.2 all-reduce.1
where the time goes:
time: 159 us
  other arithmetic  48.5 us (31%)
  local copies, waits for them, and re-layouts  33.8 us (21%)
  blocking collectives  32.1 us (20%)
  waiting for transfers between devices  20.9 us (13%)
  between operations  14.3 us (9%)
  starting transfers between devices  9.52 us (6%)
    another operation x1, other arithmetic, body(): rank = jnp.cumsum(owned_grid.astype(jnp.int32), axis=1) - 1  23.6 us
    all_gather x1, blocking collectives, body(): every_id = lax.all_gather(token_ids, 'dp', axis=0, tiled=True)  22.6 us
    all_to_all x1, waiting for transfers between devices, body(): lax.all_to_all(grad_send, 'dp', split_axis=0, concat_axis=0, tiled=True)  20.9 us
    unnamed x11, local copies, waits for them, and re-layouts  11.1 us
    scatter-add x1, other arithmetic, body(): accum = jnp.zeros((lines, width), jnp.float32).at[target.reshape(-1)].add...  10 us
    all_gather x1, blocking collectives, body(): whole_grad = lax.all_gather(out_grad, 'segment', axis=1, tiled=True)  9.52 us
    convert_element_type x1, other arithmetic, body(): return (embedded, accum.astype(jnp.bfloat16))  9.14 us
    gather x1, local copies, waits for them, and re-layouts, body(): jnp.take(table, row_of.reshape(-1), axis=0).reshape(groups, capacity, width)  6.55 us
  transfers between devices with their start and end apart: 3, of which 1 were waited for; matrix products, arithmetic and copies ran while one was open for 24% of the time, Pallas kernels for 0%

commit v1 on v0

--- a/solution.py
+++ b/solution.py
@@ -20,7 +20,8 @@
     in_section = (local >= 0) & (local < lines * PACK)
     owned = in_section & (local % PACK == slot)
     line_idx = jnp.clip(local // PACK, 0, lines - 1)
-    whole_grad = lax.all_gather(out_grad, "segment", axis=1, tiled=True)
+    pieces = lax.all_gather(out_grad, "segment", axis=0, tiled=False)
+    whole_grad = jnp.concatenate(pieces, axis=1)
     capacity = tok_rows // PACK
     owned_grid = owned.reshape(groups, tok_rows)
     rank = jnp.cumsum(owned_grid.astype(jnp.int32), axis=1) - 1

time: 159 us -> 160 us (level)
    unnamed x11 -> x12, local copies, waits for them, and re-layouts: 11.1 us -> 11.2 us
where the time goes in v1:
time: 160 us
  other arithmetic  48.5 us (30%)
  local copies, waits for them, and re-layouts  34.6 us (22%)
  blocking collectives  32.1 us (20%)
  waiting for transfers between devices  20.9 us (13%)
  between operations  14.3 us (9%)
  starting transfers between devices  9.52 us (6%)
    another operation x1, other arithmetic, body(): rank = jnp.cumsum(owned_grid.astype(jnp.int32), axis=1) - 1  23.6 us
    all_gather x1, blocking collectives, body(): every_id = lax.all_gather(token_ids, 'dp', axis=0, tiled=True)  22.6 us
    all_to_all x1, waiting for transfers between devices, body(): lax.all_to_all(grad_send, 'dp', split_axis=0, concat_axis=0, tiled=True)  20.9 us
    unnamed x12, local copies, waits for them, and re-layouts  11.2 us
    scatter-add x1, other arithmetic, body(): accum = jnp.zeros((lines, width), jnp.float32).at[target.reshape(-1)].add...  10 us
    all_gather x1, blocking collectives, body(): pieces = lax.all_gather(out_grad, 'segment', axis=0, tiled=False)  9.52 us
    convert_element_type x1, other arithmetic, body(): return (embedded, accum.astype(jnp.bfloat16))  9.14 us
    gather x1, local copies, waits for them, and re-layouts, body(): jnp.take(table, row_of.reshape(-1), axis=0).reshape(groups, capacity, width)  6.55 us
  transfers between devices with their start and end apart: 3, of which 1 were waited for; matrix products, arithmetic and copies ran while one was open for 24% of the time, Pallas kernels for 0%

profile of v1, /device:TPU:0, one launch (start us, length us, event | category | flops | bytes accessed | tf_op | source)
XLA Modules:
  0.0 159.9 jit_solution(10123239750079881271)
XLA Ops:
  7.2 0.0 copy-start.1
  7.2 0.0 copy-start
  7.2 22.6 %all-gather.1 = s32[8,1,128]{2,1,0:T(1,128)S(1)} all-gather(s32[1,1,128]{2,1,0:T(1,128)} %bitcast.46), channel_id=1, replica_groups=mesh['segment'=4,'dp'=8] {'dp'}, dimensions={0}, use_global_device_ids=true | all-gather | bytes 4608 | tf_op jit(solution)/shard_map/all_gather | solution.py:18
  29.8 0.3 copy.15
  30.1 0.3 copy.16
  30.4 23.6 %compare_select_fusion = s32[8,128,1]{2,0,1:T(8,128)S(1)} fusion(pred[8,128,1]{2,0,1:T(8,128)(4,1)S(1)} %copy.16, s32[8,128,1]{2,0,1:T(8,128)S(1)} %copy.15), kind=kOutput, calls=%fused_computation.12 | output fusion | flops 135168 | bytes 9216 | tf_op jit(solution)/shard_map/jit(cumsum)/reduce_window_sum | solution.py:27
  54.0 0.2 copy.17
  54.2 0.8 multiply_reduce_fusion
  55.0 0.1 copy.23
  55.1 0.7 and_reduce_fusion
  55.8 0.1 copy.22
  56.0 4.3 %scatter_custom_fusion.4 = s32[128]{0:T(128)S(1)} fusion(s32[1024]{0:T(1024)S(1)} %bitcast.47, s32[1024]{0:T(1024)S(1)} %fusion.6, s32[]{:T(128)} %constant.70.clone.1), kind=kCustom, calls=%fused_computation.66 | custom fusion | bytes 516
  60.3 0.1 reshape.197
  60.4 4.3 %scatter_custom_fusion.3 = pred[128]{0:T(512)(128)(4,1)S(1)} fusion(s32[1024]{0:T(1024)S(1)} %bitcast.48, pred[1024]{0:T(1024)(128)(4,1)S(1)} %broadcast.224, pred[]{:T(512)} %constant.71.clone.1), kind=kCustom, calls=%fused_computation.56 | custom fusion | bytes 129
  64.8 0.1 reshape.193
  64.9 6.6 %gather_fusion = bf16[128,3584]{1,0:T(8,128)(2,1)S(1)} fusion(bf16[1188,3584]{1,0:T(8,128)(2,1)} %param.6, s32[1024]{0:T(1024)S(1)} %pad_clamp_fusion.2), kind=kCustom, calls=%fused_computation.2 | custom fusion | bytes 1835520 | tf_op jit(solution)/shard_map/jit(_take)/gather | solution.py:36
  71.4 1.1 select_select_fusion
  72.6 3.6 %all-to-all-start = ((bf16[8,16,3584]{2,1,0:T(8,128)(2,1)}), bf16[8,16,3584]{2,1,0:T(8,128)(2,1)S(1)}, u32[]{:S(2)}, u32[]{:S(2)}) async-start(bf16[8,16,3584]{2,1,0:T(8,128)(2,1)} %select_select_fusion), calls=%async_computation | async-start | bytes 1835008 | tf_op jit(solution)/shard_map/all_to_all | solution.py:38
  76.1 0.0 copy-done.1
  76.2 0.1 fusion.4
  76.3 0.2 reduce_window_sum.23
  76.4 0.2 select_reduce_fusion
  76.7 6.4 %scatter_fusion.1 = s32[8,16]{1,0:T(8,128)S(1)} fusion(s32[8,16]{1,0:T(8,128)S(1)} %broadcast.169, s32[128]{0:T(128)S(1)} %fusion.18, s32[128]{0:T(128)S(1)} %iota.14), kind=kCustom, calls=%fused_computation.4 | custom fusion | bytes 2560 | tf_op jit(solution)/shard_map/scatter | solution.py:55
  83.0 0.1 reshape.188
  83.1 0.0 copy-done
  83.2 9.5 %all-gather = bf16[512,896]{1,0:T(8,128)(2,1)S(1)} all-gather(bf16[128,896]{1,0:T(8,128)(2,1)S(1)} %copy-done), channel_id=2, replica_groups=mesh['segment'=4,'dp'=8] {'segment'}, dimensions={0}, use_global_device_ids=true | all-gather | bytes 1146880 | tf_op jit(solution)/shard_map/all_gather | solution.py:23
  92.7 0.7 copy.21
  93.4 0.1 copy.24
  93.5 1.1 gather_fusion.2
  94.7 6.5 %scatter_fusion = pred[8,16]{1,0:T(8,128)(4,1)S(1)} fusion(pred[8,16]{1,0:T(8,128)(4,1)S(1)} %broadcast.166, s32[128]{0:T(128)S(1)} %fusion.18, pred[128]{0:T(512)(128)(4,1)S(1)} %broadcast.225), kind=kCustom, calls=%fused_computation.3 | custom fusion | bytes 1408 | tf_op jit(solution)/shard_map/scatter | solution.py:57
  101.1 0.2 broadcast_select_fusion
  101.3 1.1 broadcast_select_fusion.1
  102.4 0.0 all-to-all-done
  102.4 5.9 %all-to-all-start.1 = ((bf16[8,16,3584]{2,1,0:T(8,128)(2,1)}), bf16[8,16,3584]{2,1,0:T(8,128)(2,1)S(1)}, u32[]{:S(2)}, u32[]{:S(2)}) async-start(bf16[8,16,3584]{2,1,0:T(8,128)(2,1)} %broadcast_select_fusion.1), calls=%async_computation.1 | async-start | bytes 1835008 | tf_op jit(solution)/shard_map/all_to_all | solution.py:63
  108.3 0.0 all-reduce.2.cloned.1.call-start
  108.4 1.1 gather_fusion.1
  109.5 1.3 select_convert_fusion
  110.8 0.0 all-reduce.2.cloned.1.call-update
  110.8 0.1 reshape.185
  110.9 20.9 %all-to-all-done.1 = bf16[8,16,3584]{2,1,0:T(8,128)(2,1)S(1)} async-done(((bf16[8,16,3584]{2,1,0:T(8,128)(2,1)}), bf16[8,16,3584]{2,1,0:T(8,128)(2,1)S(1)}, u32[]{:S(2)}, u32[]{:S(2)}) %all-to-all-start.1) | async-done | bytes 917536 | tf_op jit(solution)/shard_map/all_to_all | solution.py:63
  131.7 10.0 %scatter_custom_fusion.2 = f32[1188,3584]{1,0:T(8,128)} fusion(s32[128]{0:T(128)S(1)} %fusion.16, f32[]{:T(128)} %constant.121.clone.1, bf16[128,3584]{1,0:T(8,128)(2,1)S(1)} %bitcast.42), kind=kCustom, calls=%fused_computation.8 | custom fusion | flops 917504 | bytes 17948676 | tf_op jit(solution)/shard_map/scatter-add | solution.py:68
  141.8 9.1 %convert_element_type.32 = bf16[1188,3584]{1,0:T(8,128)(2,1)} convert(f32[1188,3584]{1,0:T(8,128)} %scatter_custom_fusion.2) | non-fusion elementwise | flops 4257792 | bytes 25546752 | tf_op jit(solution)/shard_map/convert_element_type | solution.py:71
  150.9 0.0 all-reduce.2.cloned.1.call-done
  150.9 2.2 %copy.28 = bf16[128,3584]{1,0:T(8,128)(2,1)} copy(bf16[128,3584]{1,0:T(8,128)(2,1)} %all-reduce.2.cloned.1.call-done) | data formatting | bytes 1835008
  (24 shorter events, 0.2 us)
Async XLA Ops:
  7.2 69.0 %copy-start.1 = (s32[128]{0:T(128)S(1)}, s32[128]{0:T(128)}, u32[]{:S(2)}) copy-start(s32[128]{0:T(128)} %param.5) | copy-start | bytes 1540
  7.2 76.0 %copy-start = (bf16[128,896]{1,0:T(8,128)(2,1)S(1)}, bf16[128,896]{1,0:T(8,128)(2,1)}, u32[]{:S(2)}) copy-start(bf16[128,896]{1,0:T(8,128)(2,1)} %param.7) | copy-start | bytes 688132
  72.6 29.8 %all-to-all-start = ((bf16[8,16,3584]{2,1,0:T(8,128)(2,1)}), bf16[8,16,3584]{2,1,0:T(8,128)(2,1)S(1)}, u32[]{:S(2)}, u32[]{:S(2)}) async-start(bf16[8,16,3584]{2,1,0:T(8,128)(2,1)} %select_select_fusion), calls=%async_computation | async-start | bytes 1835008 | tf_op jit(solution)/shard_map/all_to_all | solution.py:38
  102.4 29.4 %all-to-all-start.1 = ((bf16[8,16,3584]{2,1,0:T(8,128)(2,1)}), bf16[8,16,3584]{2,1,0:T(8,128)(2,1)S(1)}, u32[]{:S(2)}, u32[]{:S(2)}) async-start(bf16[8,16,3584]{2,1,0:T(8,128)(2,1)} %broadcast_select_fusion.1), calls=%async_computation.1 | async-start | bytes 1835008 | tf_op jit(solution)/shard_map/all_to_all | solution.py:63
  108.3 42.6 %all-reduce.2.cloned.1.call-start = ((), (), s32[]{:S(2)}) async-start(), calls=%async_computation.2 | async-start | bytes 1835008 | tf_op jit(solution)/shard_map/psum | solution.py:70
Sparse Core Ops, SparseCore 0:
  112.0 36.2 all-reduce.1
